TPU v7x, 256 devices: a whole 4x4x8 slice. The times are simulated.
256 devices in a mesh: dp: 32 (over z_lo, x, core), mp: 8 (over z_hi, y).
Axes of the slice: x: 4, y: 4, z: 8 (z_hi: 2, z_lo: 4; z = z_hi * 4 + z_lo), core: 2. Of those that a mesh axis runs over, the one named last changes fastest.
Arguments:
- queries: bfloat16 [24576, 1024], P('dp', 'mp'), may hold values from -3 to 3
- passages: bfloat16 [24576, 1024], P('dp', 'mp'), may hold values from -3 to 3
- positive: int32 [24576], P('dp'), may hold values from 0 to 24575
Outputs:
- grad_queries: bfloat16 [24576, 1024], P('dp', 'mp')
- grad_passages: bfloat16 [24576, 1024], P('dp', 'mp')
All inputs are finite; a program needn't handle non-finite values.
Results may differ from a plain program's by a relative error of at most 0.0034.
Values may be sent and summed in bfloat16 or wider, within the bound.
A program may use at most 128 MiB of HBM per device.

v0:
```python
import math
import jax
import jax.numpy as jnp
from jax import lax
from jax.sharding import Mesh
from jax.sharding import PartitionSpec as P

MP = ("mp_0", "mp_1")


def sent_to_all(array, axis):
    copies = jnp.broadcast_to(array, (lax.axis_size(axis), *array.shape))
    return lax.all_to_all(copies, axis, split_axis=0, concat_axis=0, tiled=True)


def collected_together(array, axis):
    leaves = jax.tree.leaves(array)
    turns = sorted(range(len(leaves)), key=lambda k: -leaves[k].size)
    width = (1, *leaves[turns[0]].shape)[-1]
    lines = [
        jnp.pad(leaves[k].reshape(-1), (0, -leaves[k].size % width)).reshape(-1, width)
        for k in turns
    ]
    both, at, found = (sent_to_all(jnp.concatenate(lines), axis), 0, {})
    for k, line in zip(turns, lines):
        slab = both[:, at : at + len(line)].reshape(len(both), -1)
        found[k] = slab[:, : leaves[k].size].reshape(-1, *leaves[k].shape)
        at += len(line)
    numbers = iter(range(len(leaves)))
    return jax.tree.map(lambda _: found[next(numbers)], array)


def joined_by_halves(pieces, combine):
    while len(jax.tree.leaves(pieces)[0]) > 1:
        pieces = jax.vmap(combine)(
            *(jax.tree.map(lambda part: part[side::2], pieces) for side in (0, 1))
        )
    return jax.tree.map(lambda part: part[0], pieces)


def joined_all(array, axis, combine):
    pieces = collected_together(array, axis)
    return joined_by_halves(pieces, combine)


def sum_in_order(pieces, axes, turns):
    shape = [lax.axis_size(a) for a in axes]
    pieces = pieces.reshape(*shape, *pieces.shape[1:])
    pieces = pieces.transpose(*turns, *range(len(axes), pieces.ndim))
    pieces = pieces.reshape(-1, *pieces.shape[len(axes) :])
    for k in turns:
        pieces = lax.psum_scatter(pieces, axes[k], scatter_dimension=0, tiled=True)
    return pieces[0]


def in_blocks(array, dim, count):
    before, after = (array.shape[:dim], array.shape[dim + 1 :])
    return jnp.moveaxis(array.reshape(*before, count, -1, *after), dim, 0)


def scatter_axes(array, axes, turns, dim):
    count = lax.axis_size(axes)
    return sum_in_order(in_blocks(array, dim, count), axes, turns)


def combine(first, second):
    highest = jnp.maximum(first[0], second[0])
    merged = first[1] * jnp.exp(first[0] - highest) + second[1] * jnp.exp(second[0] - highest)
    return (highest, merged)


def local(queries, passages, positive):
    group_rows, slice_width = queries.shape
    group_count = lax.axis_size("dp")
    model_index = lax.axis_index(MP)
    relaid = lax.all_to_all(passages, MP, split_axis=0, concat_axis=1, tiled=True)
    short_rows = relaid.shape[0]
    wide_queries = lax.all_gather(queries, MP, axis=1, tiled=True)
    passage_block = lax.all_gather(relaid, "dp", axis=0, tiled=True)
    full_width = wide_queries.shape[1]
    logit_scale = 3.0 / math.sqrt(full_width)
    scores = (
        lax.dot_general(
            wide_queries,
            passage_block,
            (((1,), (1,)), ((), ())),
            preferred_element_type=jnp.float32,
        )
        * logit_scale
    )
    local_max = jnp.max(scores, axis=1)
    local_total = jnp.sum(jnp.exp(scores - local_max[:, None]), axis=1)
    highest, row_total = joined_all((local_max, local_total), MP, combine)
    log_total = highest + jnp.log(row_total)
    column_pos = jnp.arange(group_count * short_rows, dtype=jnp.int32)
    column_ids = (
        column_pos // short_rows * group_rows + model_index * short_rows + column_pos % short_rows
    )
    onehot = (column_ids[None, :] == positive[:, None]).astype(jnp.float32)
    softmax_grad = (jnp.exp(scores - log_total[:, None]) - onehot).astype(jnp.bfloat16)
    query_terms = jnp.dot(softmax_grad, passage_block, preferred_element_type=jnp.float32)
    grad_queries = scatter_axes(query_terms, MP, (1, 0), 1).astype(jnp.bfloat16)
    summed = lax.psum_scatter(
        lax.dot_general(
            softmax_grad, wide_queries, (((0,), (0,)), ((), ())), preferred_element_type=jnp.float32
        ),
        "dp",
        scatter_dimension=0,
        tiled=True,
    )
    grad_passages = lax.all_to_all(
        summed.astype(jnp.bfloat16), MP, split_axis=1, concat_axis=0, tiled=True
    )
    return (grad_queries, grad_passages)


def solution(mesh):
    finer = Mesh(mesh.devices.reshape(mesh.shape["dp"], 2, 4), ("dp", "mp_0", "mp_1"))
    return jax.shard_map(
        local,
        mesh=finer,
        in_specs=(P("dp", MP), P("dp", MP), P("dp")),
        out_specs=(P("dp", MP), P("dp", MP)),
        check_vma=False,
    )
```

profile of v0, /device:TPU:1, one launch (start us, length us, event | category | flops | bytes accessed | tf_op | source)
XLA Modules:
  0.0 441.5 jit_solution(9130345755610493085)
XLA Ops:
  7.2 0.0 all-gather.3.cloned.1.call-start
  7.2 0.7 all-gather.3.cloned.1.call-update
  7.9 0.0 all-gather.5.cloned.1.call-start
  7.9 21.4 %all_to_all.43 = bf16[8,96,128]{2,1,0:T(8,128)(2,1)S(1)} all-to-all(bf16[8,96,128]{2,1,0:T(8,128)(2,1)} %bitcast.38), channel_id=1, replica_groups=mesh['dp'=32,'mp_0'=2,'mp_1'=4] {'mp_0','mp_1'}, dimensions={0} | all-to-all | bytes 393216 | tf_op jit(solution)/shard_map/all_to_all | solution.py:76
  29.4 0.7 copy_bitcast_fusion
  30.1 0.0 all-gather.5.cloned.1.call-update
  30.1 49.0 %all-gather.3.cloned.1.call-done = bf16[768,1024]{1,0:T(8,128)(2,1)} async-done(((bf16[768,128]{1,0:T(8,128)(2,1)}), bf16[768,1024]{1,0:T(8,128)(2,1)}) %all-gather.3.cloned.1.call-update) | async-done | bytes 1572880 | tf_op jit(solution)/shard_map/all_gather | solution.py:78
  79.1 68.8 %all-gather.5.cloned.1.call-done = bf16[3072,1024]{1,0:T(8,128)(2,1)} async-done(((bf16[96,1024]{1,0:T(8,128)(2,1)}), bf16[3072,1024]{1,0:T(8,128)(2,1)}) %all-gather.5.cloned.1.call-update) | async-done | bytes 6291472 | tf_op jit(solution)/shard_map/all_gather | solution.py:79
  147.9 7.8 %multiply_reduce_fusion = (f32[768]{0:T(1024)S(1)}, f32[768,3072]{1,0:T(8,128)S(1)}) fusion(bf16[768,1024]{1,0:T(8,128)(2,1)} %all-gather.3.cloned.1.call-done, bf16[3072,1024]{1,0:T(8,128)(2,1)} %all-gather.5.cloned.1.call-done), kind=kOutput, calls=%fused_computation.2 | convolution fusion | flops 4836555776 | bytes 17304576 | tf_op jit(solution)/shard_map/dot_general | solution.py:83
  155.7 0.0 copy-start
  155.8 0.0 copy-start.2
  155.8 3.5 copy-done
  159.3 1.7 exponential_reduce_fusion
  161.0 0.6 broadcast_in_dim.2
  161.6 7.9 %all-to-all-start.1 = ((f32[8,2,768]{2,1,0:T(2,128)}), f32[8,2,768]{2,1,0:T(2,128)S(1)}, u32[]{:S(2)}, u32[]{:S(2)}) async-start(f32[8,2,768]{2,1,0:T(2,128)} %broadcast_in_dim.2), calls=%async_computation.1 | async-start | bytes 98304 | tf_op jit(solution)/shard_map/all_to_all | solution.py:13
  169.5 0.0 reduce-scatter.4.cloned.1.call-start
  169.6 9.0 %all-to-all-done.1 = f32[8,2,768]{2,1,0:T(2,128)S(1)} async-done(((f32[8,2,768]{2,1,0:T(2,128)}), f32[8,2,768]{2,1,0:T(2,128)S(1)}, u32[]{:S(2)}, u32[]{:S(2)}) %all-to-all-start.1) | async-done | bytes 49184 | tf_op jit(solution)/shard_map/all_to_all | solution.py:13
  178.9 0.0 copy-done.2
  178.9 9.8 %convolution_bitcast_fusion = f32[96,8,8,128]{3,1,2,0:T(8,128)S(1)} fusion(bf16[3072,1024]{1,0:T(8,128)(2,1)} %all-gather.5.cloned.1.call-done, f32[768,3072]{1,0:T(8,128)} %copy-done, s32[3072]{0:T(1024)S(1)} %fusion.8, f32[768]{0:T(1024)S(1)} %add_reduce_fusion, s32[768]{0:T(1024)S(1)} %copy-done.2), kind=kOutput, calls=%fused_computation.3 | convolution fusion | flops 4845993984 | bytes 18892800 | tf_op jit(solution)/shard_map/dot_general | solution.py:101
  188.7 0.0 copy-start.1
  188.8 0.7 copy.20
  189.5 2.2 copy.14
  191.7 0.0 reduce-scatter.4.cloned.1.call-update
  191.8 0.0 reduce-scatter.8.cloned.1.call-start
  191.8 0.0 copy-done.1
  191.8 11.1 %fusion.12 = f32[3072,1024]{1,0:T(8,128)} fusion(bf16[768,1024]{1,0:T(8,128)(2,1)S(1)} %copy-done.1, f32[768,3072]{1,0:T(8,128)} %copy-done, s32[3072]{0:T(1024)S(1)} %fusion.8, f32[768]{0:T(1024)S(1)} %add_reduce_fusion, s32[768]{0:T(1024)S(1)} %copy-done.2), kind=kOutput, calls=%fused_computation.33 | convolution fusion | flops 4845993984 | bytes 23611392 | tf_op jit(solution)/shard_map/dot_general | solution.py:104
  202.9 0.0 reduce-scatter.8.cloned.1.call-update
  202.9 0.0 reduce-scatter.6.cloned.1.call-start
  203.0 25.3 %reduce-scatter.4.cloned.1.call-done = f32[2,768,128]{2,1,0:T(8,128)} async-done(((f32[8,768,128]{2,1,0:T(8,128)}), f32[2,768,128]{2,1,0:T(8,128)}) %reduce-scatter.4.cloned.1.call-update) | async-done | bytes 786448 | tf_op jit(solution)/shard_map/reduce_scatter | solution.py:52
  228.2 0.0 reduce-scatter.6.cloned.1.call-update
  228.3 164.2 %reduce-scatter.8.cloned.1.call-done = f32[96,1024]{1,0:T(8,128)} async-done(((f32[3072,1024]{1,0:T(8,128)}), f32[96,1024]{1,0:T(8,128)}) %reduce-scatter.8.cloned.1.call-update) | async-done | bytes 393232 | tf_op jit(solution)/shard_map/reduce_scatter | solution.py:103
  392.4 1.7 copy_bitcast_fusion.1
  394.1 8.7 %all-to-all-start.2 = ((bf16[96,8,128]{2,0,1:T(8,128)(2,1)}), bf16[96,8,128]{2,0,1:T(8,128)(2,1)S(1)}, u32[]{:S(2)}, u32[]{:S(2)}) async-start(bf16[96,8,128]{2,0,1:T(8,128)(2,1)} %copy_bitcast_fusion.1), calls=%async_computation.5 | async-start | bytes 393216 | tf_op jit(solution)/shard_map/all_to_all | solution.py:111
  402.8 29.8 %reduce-scatter.6.cloned.1.call-done = f32[1,768,128]{2,1,0:T(8,128)} async-done(((f32[2,768,128]{2,1,0:T(8,128)}), f32[1,768,128]{2,1,0:T(8,128)}) %reduce-scatter.6.cloned.1.call-update) | async-done | bytes 393232 | tf_op jit(solution)/shard_map/reduce_scatter | solution.py:52
  432.6 1.7 convert_bitcast_fusion.1
  434.3 0.0 all-to-all-done.2
  434.3 0.7 copy.26
  (17 shorter events, 0.4 us)
Async XLA Ops:
  7.2 71.9 %all-gather.3.cloned.1.call-start = ((), (), s32[]{:S(2)}) async-start(), calls=%async_computation.6 | async-start | bytes 1769472 | tf_op jit(solution)/shard_map/all_gather | solution.py:78
  7.9 140.0 %all-gather.5.cloned.1.call-start = ((), (), s32[]{:S(2)}) async-start(), calls=%async_computation.7 | async-start | bytes 6488064 | tf_op jit(solution)/shard_map/all_gather | solution.py:79
  155.7 3.5 copy-start
  155.8 23.2 %copy-start.2 = (s32[768]{0:T(1024)S(1)}, s32[768]{0:T(1024)}, u32[]{:S(2)}) copy-start(s32[768]{0:T(1024)} %param.5) | copy-start | bytes 9220
  161.6 17.0 %all-to-all-start.1 = ((f32[8,2,768]{2,1,0:T(2,128)}), f32[8,2,768]{2,1,0:T(2,128)S(1)}, u32[]{:S(2)}, u32[]{:S(2)}) async-start(f32[8,2,768]{2,1,0:T(2,128)} %broadcast_in_dim.2), calls=%async_computation.1 | async-start | bytes 98304 | tf_op jit(solution)/shard_map/all_to_all | solution.py:13
  169.5 58.7 %reduce-scatter.4.cloned.1.call-start = ((), (), s32[]{:S(2)}) async-start(), calls=%async_computation.8 | async-start | bytes 3932160 | tf_op jit(solution)/shard_map/reduce_scatter | solution.py:52
  188.7 3.1 copy-start.1
  191.8 200.7 %reduce-scatter.8.cloned.1.call-start = ((), (), s32[]{:S(2)}) async-start(), calls=%async_computation.10 | async-start | bytes 12976128 | tf_op jit(solution)/shard_map/reduce_scatter | solution.py:103
  202.9 229.7 %reduce-scatter.6.cloned.1.call-start = ((), (), s32[]{:S(2)}) async-start(), calls=%async_computation.9 | async-start | bytes 1179648 | tf_op jit(solution)/shard_map/reduce_scatter | solution.py:52
  394.1 40.2 %all-to-all-start.2 = ((bf16[96,8,128]{2,0,1:T(8,128)(2,1)}), bf16[96,8,128]{2,0,1:T(8,128)(2,1)S(1)}, u32[]{:S(2)}, u32[]{:S(2)}) async-start(bf16[96,8,128]{2,0,1:T(8,128)(2,1)} %copy_bitcast_fusion.1), calls=%async_computation.5 | async-start | bytes 393216 | tf_op jit(solution)/shard_map/all_to_all | solution.py:111
Sparse Core Ops, SparseCore 0:
  10.4 68.6 all-gather.2
  81.5 66.3 all-gather.4
  191.9 36.3 reduce-scatter.3
  230.7 161.7 reduce-scatter.7
  394.8 37.7 reduce-scatter.5
where the time goes:
time: 442 us
  waiting for transfers between devices  347 us (79%)
  matrix products  28.7 us (6%)
  blocking collectives  21.4 us (5%)
  starting transfers between devices  16.8 us (4%)
  between operations  13.9 us (3%)
  local copies, waits for them, and re-layouts  8.76 us (2%)
  other arithmetic  5.15 us (1%)
    reduce_scatter x1, waiting for transfers between devices, local(): lax.psum_scatter(lax.dot_general(softmax_grad, wide_queries, (((0,), (0,)...  164 us
    all_gather x1, waiting for transfers between devices, local(): passage_block = lax.all_gather(relaid, 'dp', axis=0, tiled=True)  68.8 us
    reduce_scatter x2, waiting for transfers between devices, sum_in_order(): pieces = lax.psum_scatter(pieces, axes[k], scatter_dimension=0, tiled=True)  55.1 us
    all_gather x1, waiting for transfers between devices, local(): wide_queries = lax.all_gather(queries, MP, axis=1, tiled=True)  49 us
    all_to_all x1, blocking collectives, local(): lax.all_to_all(passages, MP, split_axis=0, concat_axis=1, tiled=True)  21.4 us
    dot_general x1, matrix products, local(): lax.dot_general(softmax_grad, wide_queries, (((0,), (0,)), ((), ())), pre...  11.1 us
    dot_general x1, matrix products, local(): jnp.dot(softmax_grad, passage_block, preferred_element_type=jnp.float32)  9.83 us
    all_to_all x1, waiting for transfers between devices, sent_to_all(): return lax.all_to_all(copies, axis, split_axis=0, concat_axis=0, tiled=True)  9 us
  transfers between devices with their start and end apart: 7, of which 6 were waited for; matrix products, arithmetic and copies ran while one was open for 3% of the time, Pallas kernels for 0%

commit v1 on v0

--- a/solution.py
+++ b/solution.py
@@ -4,6 +4,7 @@
 from jax import lax
 from jax.sharding import Mesh
 from jax.sharding import PartitionSpec as P
+from jax.lax import all_to_all, axis_size
 
 MP = ("mp_0", "mp_1")
 
@@ -75,7 +76,15 @@
     model_index = lax.axis_index(MP)
     relaid = lax.all_to_all(passages, MP, split_axis=0, concat_axis=1, tiled=True)
     short_rows = relaid.shape[0]
-    wide_queries = lax.all_gather(queries, MP, axis=1, tiled=True)
+    wide_queries = jnp.concatenate(
+        all_to_all(
+            jnp.stack([queries for _ in range(axis_size(MP))], 0),
+            concat_axis=0,
+            split_axis=0,
+            axis_name=MP,
+        ),
+        axis=1,
+    )
     passage_block = lax.all_gather(relaid, "dp", axis=0, tiled=True)
     full_width = wide_queries.shape[1]
     logit_scale = 3.0 / math.sqrt(full_width)

time: 442 us -> 416 us (0.941)
  waiting for transfers between devices: 347 us -> 315 us
    all_gather x1 -> x0, waiting for transfers between devices: 49 us -> none  [local(): wide_queries = lax.all_gather(queries, MP, axis=1, tiled=True)]
    all_to_all x0 -> x1, waiting for transfers between devices: none -> 42.4 us  [local(): all_to_all(jnp.stack([queries for _ in range(axis_size(MP))], 0), concat_...]
    all_gather x1, waiting for transfers between devices: 68.8 us -> 43.3 us  [local(): passage_block = lax.all_gather(relaid, 'dp', axis=0, tiled=True)]
  transfers between devices with their start and end apart: 7 -> 7, of which waited for: 6 -> 6; matrix products, arithmetic and copies ran while one was open for 3% -> 4% of each run, Pallas kernels for 0% -> 0%
where the time goes in v1:
time: 416 us; the launch traced here: 415 us
  waiting for transfers between devices  315 us (76%)
  matrix products  28.2 us (7%)
  blocking collectives  21.4 us (5%)
  starting transfers between devices  20.5 us (5%)
  between operations  13.9 us (3%)
  local copies, waits for them, and re-layouts  11.1 us (3%)
  other arithmetic  5.15 us (1%)
    reduce_scatter x1, waiting for transfers between devices, local(): lax.psum_scatter(lax.dot_general(softmax_grad, wide_queries, (((0,), (0,)...  165 us
    reduce_scatter x2, waiting for transfers between devices, sum_in_order(): pieces = lax.psum_scatter(pieces, axes[k], scatter_dimension=0, tiled=True)  55.6 us
    all_gather x1, waiting for transfers between devices, local(): passage_block = lax.all_gather(relaid, 'dp', axis=0, tiled=True)  43.3 us
    all_to_all x1, waiting for transfers between devices, local(): all_to_all(jnp.stack([queries for _ in range(axis_size(MP))], 0), concat_...  42.4 us
    all_to_all x1, blocking collectives, local(): lax.all_to_all(passages, MP, split_axis=0, concat_axis=1, tiled=True)  21.4 us
    dot_general x1, matrix products, local(): lax.dot_general(softmax_grad, wide_queries, (((0,), (0,)), ((), ())), pre...  11 us
    dot_general x1, matrix products, local(): jnp.dot(softmax_grad, passage_block, preferred_element_type=jnp.float32)  9.83 us
    all_to_all x1, waiting for transfers between devices, sent_to_all(): return lax.all_to_all(copies, axis, split_axis=0, concat_axis=0, tiled=True)  9 us
  transfers between devices with their start and end apart: 7, of which 6 were waited for; matrix products, arithmetic and copies ran while one was open for 4% of the time, Pallas kernels for 0%

profile of v1, /device:TPU:1, one launch (start us, length us, event | category | flops | bytes accessed | tf_op | source)
XLA Modules:
  0.0 415.4 jit_solution(9041479515898635664)
XLA Ops:
  7.2 0.0 all-gather.2.cloned.1.call-start
  7.2 21.4 %all_to_all.48 = bf16[8,96,128]{2,1,0:T(8,128)(2,1)S(1)} all-to-all(bf16[8,96,128]{2,1,0:T(8,128)(2,1)} %bitcast.43), channel_id=1, replica_groups=mesh['dp'=32,'mp_0'=2,'mp_1'=4] {'mp_0','mp_1'}, dimensions={0} | all-to-all | bytes 393216 | tf_op jit(solution)/shard_map/all_to_all | solution.py:77
  28.6 0.7 copy_bitcast_fusion
  29.3 0.0 all-gather.2.cloned.1.call-update
  29.4 1.1 copy.13
  30.4 1.2 stack.2
  31.7 3.6 all-to-all-start
  35.3 42.4 %all-to-all-done = bf16[8,768,128]{1,2,0:T(8,128)(2,1)S(1)} async-done(((bf16[8,768,128]{1,2,0:T(8,128)(2,1)}), bf16[8,768,128]{1,2,0:T(8,128)(2,1)S(1)}, u32[]{:S(2)}, u32[]{:S(2)}) %all-to-all-start) | async-done | bytes 1572896 | tf_op jit(solution)/shard_map/all_to_all | solution.py:80
  77.7 43.3 %all-gather.2.cloned.1.call-done = bf16[3072,1024]{1,0:T(8,128)(2,1)} async-done(((bf16[96,1024]{1,0:T(8,128)(2,1)}), bf16[3072,1024]{1,0:T(8,128)(2,1)}) %all-gather.2.cloned.1.call-update) | async-done | bytes 6291472 | tf_op jit(solution)/shard_map/all_gather | solution.py:88
  121.0 7.4 %multiply_reduce_fusion = (f32[768]{0:T(1024)S(1)}, f32[768,3072]{1,0:T(8,128)S(1)}) fusion(bf16[768,1024]{0,1:T(8,128)(2,1)S(1)} %bitcast.40, bf16[3072,1024]{1,0:T(8,128)(2,1)} %all-gather.2.cloned.1.call-done), kind=kOutput, calls=%fused_computation.2 | convolution fusion | flops 4836555776 | bytes 17304576 | tf_op jit(solution)/shard_map/dot_general | solution.py:92
  128.3 0.0 copy-start
  128.3 0.0 copy-start.1
  128.4 3.5 copy-done
  131.9 1.7 exponential_reduce_fusion
  133.6 0.6 broadcast_in_dim.2
  134.2 8.7 %all-to-all-start.2 = ((f32[8,2,768]{2,1,0:T(2,128)}), f32[8,2,768]{2,1,0:T(2,128)S(1)}, u32[]{:S(2)}, u32[]{:S(2)}) async-start(f32[8,2,768]{2,1,0:T(2,128)} %broadcast_in_dim.2), calls=%async_computation.2 | async-start | bytes 98304 | tf_op jit(solution)/shard_map/all_to_all | solution.py:14
  142.9 0.0 reduce-scatter.4.cloned.1.call-start
  143.0 9.0 %all-to-all-done.2 = f32[8,2,768]{2,1,0:T(2,128)S(1)} async-done(((f32[8,2,768]{2,1,0:T(2,128)}), f32[8,2,768]{2,1,0:T(2,128)S(1)}, u32[]{:S(2)}, u32[]{:S(2)}) %all-to-all-start.2) | async-done | bytes 49184 | tf_op jit(solution)/shard_map/all_to_all | solution.py:14
  152.3 0.0 copy-done.1
  152.3 9.8 %convolution_bitcast_fusion = f32[96,8,8,128]{3,1,2,0:T(8,128)S(1)} fusion(bf16[3072,1024]{1,0:T(8,128)(2,1)} %all-gather.2.cloned.1.call-done, f32[768,3072]{1,0:T(8,128)} %copy-done, s32[3072]{0:T(1024)S(1)} %fusion.8, f32[768]{0:T(1024)S(1)} %add_reduce_fusion, s32[768]{0:T(1024)S(1)} %copy-done.1), kind=kOutput, calls=%fused_computation.3 | convolution fusion | flops 4845993984 | bytes 18892800 | tf_op jit(solution)/shard_map/dot_general | solution.py:110
  162.2 0.7 copy.22
  162.9 2.2 copy.16
  165.2 0.0 reduce-scatter.4.cloned.1.call-update
  165.2 0.2 reduce-scatter.8.cloned.1.call-start
  165.4 11.0 %fusion.12 = f32[3072,1024]{1,0:T(8,128)} fusion(bf16[768,1024]{0,1:T(8,128)(2,1)S(1)} %bitcast.41, f32[768,3072]{1,0:T(8,128)} %copy-done, s32[3072]{0:T(1024)S(1)} %fusion.8, f32[768]{0:T(1024)S(1)} %add_reduce_fusion, s32[768]{0:T(1024)S(1)} %copy-done.1), kind=kOutput, calls=%fused_computation.33 | convolution fusion | flops 4845993984 | bytes 23611392 | tf_op jit(solution)/shard_map/dot_general | solution.py:113
  176.5 0.0 reduce-scatter.8.cloned.1.call-update
  176.5 0.0 reduce-scatter.6.cloned.1.call-start
  176.5 25.8 %reduce-scatter.4.cloned.1.call-done = f32[2,768,128]{2,1,0:T(8,128)} async-done(((f32[8,768,128]{2,1,0:T(8,128)}), f32[2,768,128]{2,1,0:T(8,128)}) %reduce-scatter.4.cloned.1.call-update) | async-done | bytes 786448 | tf_op jit(solution)/shard_map/reduce_scatter | solution.py:53
  202.3 0.0 reduce-scatter.6.cloned.1.call-update
  202.4 164.7 %reduce-scatter.8.cloned.1.call-done = f32[96,1024]{1,0:T(8,128)} async-done(((f32[3072,1024]{1,0:T(8,128)}), f32[96,1024]{1,0:T(8,128)}) %reduce-scatter.8.cloned.1.call-update) | async-done | bytes 393232 | tf_op jit(solution)/shard_map/reduce_scatter | solution.py:112
  367.1 1.7 copy_bitcast_fusion.1
  368.8 7.9 %all-to-all-start.3 = ((bf16[96,8,128]{2,0,1:T(8,128)(2,1)}), bf16[96,8,128]{2,0,1:T(8,128)(2,1)S(1)}, u32[]{:S(2)}, u32[]{:S(2)}) async-start(bf16[96,8,128]{2,0,1:T(8,128)(2,1)} %copy_bitcast_fusion.1), calls=%async_computation.6 | async-start | bytes 393216 | tf_op jit(solution)/shard_map/all_to_all | solution.py:120
  376.7 29.8 %reduce-scatter.6.cloned.1.call-done = f32[1,768,128]{2,1,0:T(8,128)} async-done(((f32[2,768,128]{2,1,0:T(8,128)}), f32[1,768,128]{2,1,0:T(8,128)}) %reduce-scatter.6.cloned.1.call-update) | async-done | bytes 393232 | tf_op jit(solution)/shard_map/reduce_scatter | solution.py:53
  406.5 1.7 convert_bitcast_fusion.1
  408.2 0.0 all-to-all-done.3
  408.2 0.7 copy.28
  (17 shorter events, 0.4 us)
Async XLA Ops:
  7.2 113.8 %all-gather.2.cloned.1.call-start = ((), (), s32[]{:S(2)}) async-start(), calls=%async_computation.7 | async-start | bytes 6488064 | tf_op jit(solution)/shard_map/all_gather | solution.py:88
  31.7 46.0 %all-to-all-start = ((bf16[8,768,128]{1,2,0:T(8,128)(2,1)}), bf16[8,768,128]{1,2,0:T(8,128)(2,1)S(1)}, u32[]{:S(2)}, u32[]{:S(2)}) async-start(bf16[8,768,128]{1,2,0:T(8,128)(2,1)} %stack.2), calls=%async_computation | async-start | bytes 3145728 | tf_op jit(solution)/shard_map/all_to_all | solution.py:80
  128.3 3.6 copy-start
  128.3 24.0 %copy-start.1 = (s32[768]{0:T(1024)S(1)}, s32[768]{0:T(1024)}, u32[]{:S(2)}) copy-start(s32[768]{0:T(1024)} %param.5) | copy-start | bytes 9220
  134.2 17.8 %all-to-all-start.2 = ((f32[8,2,768]{2,1,0:T(2,128)}), f32[8,2,768]{2,1,0:T(2,128)S(1)}, u32[]{:S(2)}, u32[]{:S(2)}) async-start(f32[8,2,768]{2,1,0:T(2,128)} %broadcast_in_dim.2), calls=%async_computation.2 | async-start | bytes 98304 | tf_op jit(solution)/shard_map/all_to_all | solution.py:14
  142.9 59.4 %reduce-scatter.4.cloned.1.call-start = ((), (), s32[]{:S(2)}) async-start(), calls=%async_computation.8 | async-start | bytes 3932160 | tf_op jit(solution)/shard_map/reduce_scatter | solution.py:53
  165.2 201.9 %reduce-scatter.8.cloned.1.call-start = ((), (), s32[]{:S(2)}) async-start(), calls=%async_computation.10 | async-start | bytes 12976128 | tf_op jit(solution)/shard_map/reduce_scatter | solution.py:112
  176.5 230.0 %reduce-scatter.6.cloned.1.call-start = ((), (), s32[]{:S(2)}) async-start(), calls=%async_computation.9 | async-start | bytes 1179648 | tf_op jit(solution)/shard_map/reduce_scatter | solution.py:53
  368.8 39.4 %all-to-all-start.3 = ((bf16[96,8,128]{2,0,1:T(8,128)(2,1)}), bf16[96,8,128]{2,0,1:T(8,128)(2,1)S(1)}, u32[]{:S(2)}, u32[]{:S(2)}) async-start(bf16[96,8,128]{2,0,1:T(8,128)(2,1)} %copy_bitcast_fusion.1), calls=%async_computation.6 | async-start | bytes 393216 | tf_op jit(solution)/shard_map/all_to_all | solution.py:120
Sparse Core Ops, SparseCore 0:
  29.5 91.4 all-gather.1
  165.3 36.9 reduce-scatter.3
  204.9 162.1 reduce-scatter.7
  369.4 37.0 reduce-scatter.5
